TPU v7x, 32 devices: a whole 2x2x4 slice. The times are simulated.
32 devices in a mesh: tp: 32 (over z, y, x, core).
Axes of the slice: x: 2, y: 2, z: 4, core: 2. Of those that a mesh axis runs over, the one named last changes fastest.
Arguments:
- hidden: bfloat16 [3, 2048, 4096], P(None, 'tp')
- labels: int32 [3, 2048], P(None, 'tp')
- loss_mask: int32 [3, 2048], P(None, 'tp')
- norm_gain: float32 [4096], replicated
- w_head: bfloat16 [4096, 65536], P(None, 'tp')
Outputs:
- output 1: float32 [], replicated
- output 2: bfloat16 [3, 2048, 4096], P(None, 'tp')
- output 3: bfloat16 [4096, 65536], P(None, 'tp')
- output 4: float32 [4096], replicated
All inputs are finite; a program needn't handle non-finite values.
Results may differ from a plain program's by a relative error of at most 0.00839355.
Values are sent between devices in bfloat16 or wider.
A program may use at most 1 GiB of HBM per device.

v0:
```python
import jax
import jax.numpy as jnp
from jax import lax
from jax.sharding import PartitionSpec as P

NORM_EPS = 1e-6
STAGES = ((1, 64), (2, 56), (4, 40), (8, 32), (16, 24))
ROWS = (64, 56)
UNITS = ((('y', 'z', 'x'), 6), (('x', 'z', 'y'), 6), (('x', 'y', 'z'), 10), (('y', 'x', 'z'), 10))


def rms_norm(x_rows, norm_gain):
    inv_rms = lax.rsqrt(jnp.mean(x_rows * x_rows, axis=-1, keepdims=True) + NORM_EPS)
    return x_rows * inv_rms * norm_gain


def full_step(n_shards, hidden, labels, loss_mask, norm_gain, w_head):
    batch_size, seq_loc, model_width = hidden.shape
    v_loc = w_head.shape[1]
    norm_loc, norm_vjp = jax.vjp(rms_norm, hidden.astype(jnp.float32), norm_gain)
    hn_all = lax.all_gather(norm_loc.astype(jnp.bfloat16), 'tp', axis=1, tiled=True)
    label_all = lax.all_gather(labels, 'tp', axis=1, tiled=True)
    mask_all = lax.all_gather(loss_mask, 'tp', axis=1, tiled=True)
    logits = jnp.einsum('btd,dv->btv', hn_all, w_head, preferred_element_type=jnp.float32)
    row_max = lax.pmax(jnp.max(logits, axis=-1), 'tp')
    sum_exp = lax.psum(jnp.sum(jnp.exp(logits - row_max[..., None]), axis=-1), 'tp')
    col_start = lax.axis_index('tp') * v_loc
    is_label = (lax.broadcasted_iota(jnp.int32, (1, 1, v_loc), 2) + col_start) == label_all[..., None]
    label_logit = lax.psum(jnp.sum(jnp.where(is_label, logits, 0.0), axis=-1), 'tp')
    log_norm = row_max + jnp.log(sum_exp)
    tok_weight = mask_all.astype(jnp.float32)
    kept_count = jnp.sum(tok_weight)
    mean_loss = jnp.sum(tok_weight * (log_norm - label_logit)) / kept_count
    tok_scale = tok_weight / kept_count
    d_logits = ((jnp.exp(logits - log_norm[..., None]) - is_label.astype(jnp.float32)) * tok_scale[..., None]).astype(jnp.bfloat16)
    d_head = jnp.einsum('btd,btv->dv', hn_all, d_logits, preferred_element_type=jnp.float32).astype(jnp.bfloat16)
    dhn_part = jnp.einsum('btv,dv->btd', d_logits, w_head, preferred_element_type=jnp.float32).astype(jnp.bfloat16)
    received = lax.all_to_all(dhn_part.reshape(batch_size, n_shards, seq_loc, model_width), 'tp', 1, 1, tiled=True)
    d_norm = jnp.sum(received, axis=1, dtype=jnp.float32)
    d_x, d_gain = norm_vjp(d_norm)
    d_gain = lax.psum(d_gain, 'tp')
    return mean_loss, d_x.astype(jnp.bfloat16), d_head, d_gain


def solution(mesh):
    n = mesh.shape['tp']
    dims = (n // 8, 2, 2, 2)
    bits = [1 << i for i in range(n.bit_length() - 1)]

    def swap(a, flip):
        return lax.ppermute(a, 'tp', [(i, i ^ flip) for i in range(n)])

    def at(a, axis, i):
        return lax.dynamic_index_in_dim(a, i, axis, keepdims=False)

    def after(values, dep):
        return lax.optimization_barrier((values, dep))[0]

    def device_step(hidden, labels, loss_mask, norm_gain, w_head):
        f32, i32 = jnp.float32, jnp.int32
        batch_size, seq_loc, model_width = hidden.shape
        n_rows = batch_size * seq_loc
        v_loc = w_head.shape[1]
        me = lax.axis_index('tp')
        place = {'core': me & 1, 'x': (me >> 1) & 1, 'y': (me >> 2) & 1, 'z': me >> 3}
        slot = jnp.arange(n_rows, dtype=i32)

        mask = loss_mask.reshape(n_rows)
        pos = jnp.cumsum(mask) - 1
        all_slots = jnp.arange(n_rows, dtype=i32)
        chosen = (pos[None, :] == all_slots[:, None]) & (mask[None, :] == 1)
        order = jnp.sum(jnp.where(chosen, all_slots[None, :], 0), axis=1)
        packed_lab = jnp.sum(jnp.where(chosen, labels.reshape(n_rows)[None, :] + 1, 0), axis=1) - 1
        packed = jnp.take(hidden.reshape(n_rows, model_width), order, axis=0, mode='clip')
        count = jnp.maximum(jnp.sum(mask) - ROWS[0], 0)
        n_rest = n_rows - ROWS[0]
        slot = jnp.arange(n_rest, dtype=i32)

        def normed(x_rows):
            out, vjp = jax.vjp(rms_norm, x_rows.astype(f32), norm_gain)
            out = out.astype(jnp.bfloat16)
            return lax.all_gather(out, 'tp', axis=0, tiled=True), vjp, out

        hn, vjps = [None, None], [None, None]
        hn[0], vjps[0], sent = normed(packed[:ROWS[0]])
        rows, lab = after((packed[ROWS[0]:], packed_lab[ROWS[0]:]), sent)
        fits = jnp.bool_(True)
        moves = []
        for bit, cap in STAGES:
            start = jnp.maximum(count - cap, 0)
            ints = jnp.concatenate([lax.dynamic_slice_in_dim(lab, start, cap), jnp.full((128,), count, i32)])
            got_rows = swap(lax.dynamic_slice_in_dim(rows, start, cap), bit)
            got_ints = swap(ints, bit)
            other = got_ints[cap]
            upper = (me & bit) // bit
            target = (count + other + 1 - upper) >> 1
            fits = fits & (jnp.abs(target - count) <= cap)
            first = count + other - target - jnp.maximum(other - cap, 0)
            src = jnp.where(slot < count, slot, n_rest + jnp.clip(first + slot - count, 0, cap - 1))
            rows = jnp.take(jnp.concatenate([rows, got_rows]), src, axis=0, mode='clip')
            lab = jnp.take(jnp.concatenate([lab, got_ints[:cap]]), src, axis=0, mode='clip')
            moves.append((bit, cap, count, other, target))
            count = target
        fits = fits & (count <= ROWS[1])
        hn[1], vjps[1], _ = normed(rows[:ROWS[1]])
        lab = jnp.where(slot < count, lab, -1)[:ROWS[1]]
        rows_all = sum(ROWS)
        known = lax.all_gather(jnp.concatenate([packed_lab[:ROWS[0]], lab, jnp.full((128,), fits.astype(i32))]), 'tp', axis=0, tiled=False)
        all_fit = jnp.min(known[:, rows_all]) == 1
        label_all = [k.reshape(-1) for k in jnp.split(known[:, :rows_all], [ROWS[0]], axis=1)]
        weight = [(lb >= 0).astype(f32) for lb in label_all]
        kept_count = sum(jnp.sum(w) for w in weight)
        cols = lax.broadcasted_iota(i32, (1, v_loc), 1) + me * v_loc

        def forward(c):
            lg = jnp.einsum('td,dv->tv', hn[c], w_head, preferred_element_type=f32)
            lg = lax.optimization_barrier(lg)
            row_max = jnp.max(lg, axis=-1)
            row_sum = jnp.sum(jnp.exp(lg - row_max[:, None]), axis=-1)
            row_lab = jnp.sum(jnp.where(cols == label_all[c][:, None], lg, 0.0), axis=-1)
            return lg, jnp.stack([row_max, row_sum, row_lab])

        def combine_all(mine):
            for bit in bits:
                theirs = swap(mine, bit)
                upper = (me & bit) != 0
                lo, hi = jnp.where(upper, theirs, mine), jnp.where(upper, mine, theirs)
                top = jnp.maximum(lo[0], hi[0])
                mine = jnp.stack([top, lo[1] * jnp.exp(lo[0] - top) + hi[1] * jnp.exp(hi[0] - top), lo[2] + hi[2]])
            return mine[0] + jnp.log(mine[1]), mine[2]

        def softmax_grad(c, lg, log_norm):
            is_label = (cols == label_all[c][:, None]).astype(f32)
            scale = weight[c] / kept_count
            return ((jnp.exp(lg - log_norm[:, None]) - is_label) * scale[:, None]).astype(jnp.bfloat16)

        class Reduce:
            def __init__(self, part, path, per):
                part = part.reshape(*dims, per, -1)
                step = {'x': 2, 'y': 4}
                a, self.second_axis, self.third_axis = path
                a_axis = {'y': 1, 'x': 2}[a]
                self.bit = {**step, 'z': 8}

                def group(da, dc):
                    return at(at(part, 3, place['core'] ^ dc), a_axis, place[a] ^ da)

                self.sent = [group(1, 0), group(1, 1), group(0, 1)]
                self.terms = [group(0, 0)]
                self.terms += [swap(g, f) for g, f in zip(self.sent, (step[a], step[a] | 1, 1))]

            def _exchange(self, pick, name):
                size = dims[0] if name == 'z' else 2
                self.sent = [pick(place[name] ^ d) for d in range(1, size)]
                self.terms = [pick(place[name])]
                self.terms += [swap(g, self.bit[name] * d) for d, g in enumerate(self.sent, 1)]
                return self.sent

            def second(self, dep):
                terms, name = after(self.terms, dep), self.second_axis
                axis = 0 if name == 'z' else 1
                return self._exchange(lambda i: sum(at(t, axis, i).astype(f32) for t in terms), name)

            def third(self, dep):
                terms = after(self.terms, dep)
                return self._exchange(lambda i: sum(at(t, 0, i) for t in terms), self.third_axis)

            def last(self, dep):
                return sum(after(self.terms, dep))

        d_logits, log_norm, label_logit, units = {}, {}, {}, {}

        def hidden_grad(c, u, dep):
            low = sum(w for _, w in UNITS[:u]) * model_width // 32
            path, w = UNITS[u]
            dl, w_part = after(d_logits[c], dep), w_head[low:low + w * model_width // 32]
            part = jnp.einsum('tv,dv->td', dl, w_part, preferred_element_type=f32).astype(jnp.bfloat16)
            units[c, u] = Reduce(part, path, ROWS[c])
            return units[c, u].sent

        def head_grad(c, acc, dep):
            dl = after(d_logits[c], dep)
            term = jnp.einsum('td,tv->dv', hn[c], dl, preferred_element_type=f32)
            return term if acc is None else acc + term

        nu = len(UNITS)
        lg0, st0 = forward(0)
        log_norm[0], label_logit[0] = combine_all(st0)
        d_logits[0] = dep = softmax_grad(0, lg0, log_norm[0])
        for u in range(nu):
            dep = hidden_grad(0, u, dep)
        dep = units[0, 0].second(dep)
        dep = units[0, 1].second(dep)
        hn[1] = after(hn[1], dep)
        lg1, st1 = forward(1)
        log_norm[1], label_logit[1] = combine_all(st1)
        dep = units[0, 2].second(log_norm[1])
        dep = units[0, 3].second(dep)
        dep = units[0, 0].third(dep)
        dep = units[0, 1].third(dep)
        d_logits[1] = dep = softmax_grad(1, after(lg1, dep), log_norm[1])
        dep = hidden_grad(1, 0, dep)
        dep = hidden_grad(1, 1, dep)
        dep = units[0, 2].third(dep)
        dep = units[0, 3].third(dep)
        dep = hidden_grad(1, 2, dep)
        dep = hidden_grad(1, 3, dep)
        dep = units[1, 0].second(dep)
        dep = units[1, 1].second(dep)
        head = dep = head_grad(0, None, dep)
        dep = units[1, 2].second(dep)
        dep = units[1, 3].second(dep)
        early = vjps[0](jnp.concatenate([units[0, u].last(dep) for u in range(nu)], axis=-1))
        dep = early = early[0].astype(jnp.bfloat16), early[1]
        for u in range(nu):
            dep = units[1, u].third(dep)
        d_head = dep = head_grad(1, head, dep).astype(jnp.bfloat16)
        late = vjps[1](jnp.concatenate([units[1, u].last(dep) for u in range(nu)], axis=-1))
        d_x, d_gain = (early[0], late[0].astype(jnp.bfloat16)), early[1] + late[1]
        loss = sum(jnp.sum(weight[c] * (log_norm[c] - label_logit[c])) for c in range(2))
        mean_loss = loss / kept_count
        for bit in bits:
            d_gain = d_gain + swap(d_gain, bit)

        back = jnp.concatenate([d_x[1], jnp.zeros((n_rest - ROWS[1], model_width), jnp.bfloat16)])
        for bit, cap, count, other, target in reversed(moves):
            got = swap(lax.dynamic_slice_in_dim(back, jnp.minimum(count, n_rest - cap), cap), bit)
            first = jnp.maximum(other - (n_rest - cap), 0)
            src = jnp.where(slot < target, slot, n_rest + jnp.clip(first + slot - target, 0, cap - 1))
            back = jnp.take(jnp.concatenate([back, got]), src, axis=0, mode='clip')
        back = jnp.take(jnp.concatenate([d_x[0], back]), pos, axis=0, mode='clip')
        d_hidden = jnp.where(mask[:, None] == 1, back, jnp.zeros((), jnp.bfloat16)).reshape(hidden.shape)

        def every_token(_):
            return (jnp.bool_(True), *full_step(n, hidden, labels, loss_mask, norm_gain, w_head))

        return lax.while_loop(lambda c: ~c[0], every_token, (all_fit, mean_loss, d_hidden, d_head, d_gain))[1:]

    return jax.shard_map(device_step, mesh=mesh, in_specs=(P(None, 'tp', None), P(None, 'tp'), P(None, 'tp'), P(), P(None, 'tp')), out_specs=(P(), P(None, 'tp', None), P(None, 'tp'), P()), check_vma=False)
```

profile of v0, /device:TPU:0, one launch (start us, length us, event | category | flops | bytes accessed | tf_op | source)
XLA Modules:
  0.0 924.9 jit_solution(6747446898380789484)
XLA Ops:
  29.6 13.2 %collective-permute-done.1 = s32[184]{0:T(256)S(1)} collective-permute-done((s32[184]{0:T(256)S(1)}, s32[184]{0:T(256)S(1)}, u32[]{:S(2)}, u32[]{:S(2)}) %collective-permute-start.1) | collective-permute-done | bytes 768 | tf_op jit(solution)/shard_map/ppermute | solution.py:51
  89.3 20.9 %collective-permute-done.14 = bf16[24,4096]{1,0:T(8,128)(2,1)S(1)} collective-permute-done((bf16[24,4096]{1,0:T(8,128)(2,1)S(1)}, bf16[24,4096]{1,0:T(8,128)(2,1)S(1)}, u32[]{:S(2)}, u32[]{:S(2)}) %collective-permute-start.14) | collective-permute-done | bytes 196640 | tf_op jit(solution)/shard_map/ppermute | solution.py:51
  115.1 43.8 %all-reduce.7 = s32[7936]{0:T(1024)S(1)} all-reduce(s32[7936]{0:T(1024)S(1)} %add_dynamic-update-slice_fusion), channel_id=2, replica_groups=mesh['tp'=32] {'tp'}, use_global_device_ids=true, to_apply=%add.7 | all-reduce | flops 7936 | bytes 63488
  159.1 43.1 %fusion.80 = f32[2048,2048]{1,0:T(8,128)} fusion(bf16[2048,4096]{1,0:T(8,128)(2,1)} %all-gather.9.cloned.1.call-done, bf16[4096,2048]{1,0:T(8,128)(2,1)} %param.11), kind=kOutput, calls=%fused_computation.394 | convolution fusion | flops 34359738368 | bytes 50331648 | tf_op jit(solution)/shard_map/td,dv->tv/dot_general | solution.py:116
  254.5 11.7 %convolution_convert_fusion.6 = bf16[2048,768]{1,0:T(8,128)(2,1)S(1)} fusion(bf16[2048,2048]{1,0:T(8,128)(2,1)S(1)} %fusion.21, bf16[4096,2048]{1,0:T(8,128)(2,1)} %param.11), kind=kOutput, calls=%fused_computation.75 | convolution fusion | flops 6444023808 | bytes 14680064 | tf_op jit(solution)/shard_map/tv,dv->td/dot_general | solution.py:177
  281.1 13.7 %convolution_convert_fusion.4 = bf16[2048,1280]{1,0:T(8,128)(2,1)S(1)} fusion(bf16[2048,2048]{1,0:T(8,128)(2,1)S(1)} %fusion.21, bf16[4096,2048]{1,0:T(8,128)(2,1)} %param.11), kind=kOutput, calls=%fused_computation.69 | convolution fusion | flops 10740039680 | bytes 18874368 | tf_op jit(solution)/shard_map/tv,dv->td/dot_general | solution.py:177
  299.9 13.9 %convolution_convert_fusion.3 = bf16[2048,1280]{1,0:T(8,128)(2,1)S(1)} fusion(bf16[2048,2048]{1,0:T(8,128)(2,1)S(1)} %fusion.21, bf16[4096,2048]{1,0:T(8,128)(2,1)} %param.11), kind=kOutput, calls=%fused_computation.68 | convolution fusion | flops 10740039680 | bytes 18874368 | tf_op jit(solution)/shard_map/tv,dv->td/dot_general | solution.py:177
  323.7 38.2 %fusion.81 = f32[1792,2048]{1,0:T(8,128)} fusion(bf16[1792,4096]{1,0:T(8,128)(2,1)} %all-gather.11.cloned.1.call-done, bf16[4096,2048]{1,0:T(8,128)(2,1)} %param.11), kind=kOutput, calls=%fused_computation.395 | convolution fusion | flops 30064771072 | bytes 46137344 | tf_op jit(solution)/shard_map/td,dv->tv/dot_general | solution.py:116
  395.4 20.3 %collective-permute-done.32 = bf16[4,2,64,1280]{3,2,0,1:T(8,128)(2,1)S(1)} collective-permute-done((bf16[4,2,64,1280]{3,2,0,1:T(8,128)(2,1)S(1)}, bf16[4,2,64,1280]{3,2,0,1:T(8,128)(2,1)S(1)}, u32[]{:S(2)}, u32[]{:S(2)}) %collective-permute-start.32) | collective-permute-done | bytes 1310752 | tf_op jit(solution)/shard_map/ppermute | solution.py:51
  416.4 22.9 %collective-permute-done.33 = bf16[4,2,64,1280]{3,2,0,1:T(8,128)(2,1)S(1)} collective-permute-done((bf16[4,2,64,1280]{3,2,0,1:T(8,128)(2,1)S(1)}, bf16[4,2,64,1280]{3,2,0,1:T(8,128)(2,1)S(1)}, u32[]{:S(2)}, u32[]{:S(2)}) %collective-permute-start.33) | collective-permute-done | bytes 1310752 | tf_op jit(solution)/shard_map/ppermute | solution.py:51
  452.1 15.6 %collective-permute-start.36 = (f32[2,64,768]{2,1,0:T(8,128)S(1)}, f32[2,64,768]{2,1,0:T(8,128)S(1)}, u32[]{:S(2)}, u32[]{:S(2)}) collective-permute-start(f32[2,64,768]{2,1,0:T(8,128)S(1)} %get-tuple-element.345), channel_id=1, source_target_pairs={{0,8},{1,9},{2,10},{3,11},{4,12},{5,13},{6,14},{7,15},{8,0},{9,1},... | collective-permute-start | bytes 1179656 | tf_op jit(solution)/shard_map/ppermute | solution.py:51
  468.3 24.1 %collective-permute-done.27 = f32[2,64,768]{2,1,0:T(8,128)S(1)} collective-permute-done((f32[2,64,768]{2,1,0:T(8,128)S(1)}, f32[2,64,768]{2,1,0:T(8,128)S(1)}, u32[]{:S(2)}, u32[]{:S(2)}) %collective-permute-start.27) | collective-permute-done | bytes 393248 | tf_op jit(solution)/shard_map/ppermute | solution.py:51
  496.3 13.0 %collective-permute-done.37 = f32[2,64,768]{2,1,0:T(8,128)S(1)} collective-permute-done((f32[2,64,768]{2,1,0:T(8,128)S(1)}, f32[2,64,768]{2,1,0:T(8,128)S(1)}, u32[]{:S(2)}, u32[]{:S(2)}) %collective-permute-start.37) | collective-permute-done | bytes 393248 | tf_op jit(solution)/shard_map/ppermute | solution.py:51
  542.8 12.4 %convolution_convert_fusion.2 = bf16[1792,1280]{1,0:T(8,128)(2,1)S(1)} fusion(bf16[1792,2048]{1,0:T(8,128)(2,1)S(1)} %fusion.25, bf16[4096,2048]{1,0:T(8,128)(2,1)} %param.11), kind=kOutput, calls=%fused_computation.67 | convolution fusion | flops 9397534720 | bytes 17170432 | tf_op jit(solution)/shard_map/tv,dv->td/dot_general | solution.py:177
  561.4 12.4 %convolution_convert_fusion.1 = bf16[1792,1280]{1,0:T(8,128)(2,1)S(1)} fusion(bf16[1792,2048]{1,0:T(8,128)(2,1)S(1)} %fusion.25, bf16[4096,2048]{1,0:T(8,128)(2,1)} %param.11), kind=kOutput, calls=%fused_computation.66 | convolution fusion | flops 9397534720 | bytes 17170432 | tf_op jit(solution)/shard_map/tv,dv->td/dot_general | solution.py:177
  586.6 11.0 %collective-permute-start.57 = (f32[64,1280]{1,0:T(8,128)}, f32[64,1280]{1,0:T(8,128)}, u32[]{:S(2)}, u32[]{:S(2)}) collective-permute-start(f32[64,1280]{1,0:T(8,128)} %get-tuple-element.377), channel_id=1, source_target_pairs={{0,8},{1,9},{2,10},{3,11},{4,12},{5,13},{6,14},{7,15},{8,0},{9,1},... | collective-permute-start | bytes 983048 | tf_op jit(solution)/shard_map/ppermute | solution.py:51
  601.9 22.8 %collective-permute-done.45 = bf16[4,2,56,1280]{3,2,0,1:T(8,128)(2,1)} collective-permute-done((bf16[4,2,56,1280]{3,2,0,1:T(8,128)(2,1)}, bf16[4,2,56,1280]{3,2,0,1:T(8,128)(2,1)}, u32[]{:S(2)}, u32[]{:S(2)}) %collective-permute-start.45) | collective-permute-done | bytes 1146912 | tf_op jit(solution)/shard_map/ppermute | solution.py:51
  625.8 42.5 %fusion.82 = f32[4096,2048]{1,0:T(8,128)} fusion(bf16[2048,4096]{1,0:T(8,128)(2,1)} %all-gather.9.cloned.1.call-done, bf16[2048,2048]{1,0:T(8,128)(2,1)S(1)} %bitcast.276), kind=kOutput, calls=%fused_computation.396 | convolution fusion | flops 34359738368 | bytes 58720256 | tf_op jit(solution)/shard_map/td,tv->dv/dot_general | solution.py:183
  683.4 23.1 %collective-permute-done.55 = f32[64,1280]{1,0:T(8,128)S(1)} collective-permute-done((f32[64,1280]{1,0:T(8,128)S(1)}, f32[64,1280]{1,0:T(8,128)S(1)}, u32[]{:S(2)}, u32[]{:S(2)}) %collective-permute-start.55) | collective-permute-done | bytes 327712 | tf_op jit(solution)/shard_map/ppermute | solution.py:51
  713.6 11.8 %collective-permute-done.62 = f32[2,56,768]{2,1,0:T(8,128)S(1)} collective-permute-done((f32[2,56,768]{2,1,0:T(8,128)S(1)}, f32[2,56,768]{2,1,0:T(8,128)S(1)}, u32[]{:S(2)}, u32[]{:S(2)}) %collective-permute-start.62) | collective-permute-done | bytes 344096 | tf_op jit(solution)/shard_map/ppermute | solution.py:51
  725.3 26.0 %collective-permute-start.66 = (f32[2,56,768]{2,1,0:T(8,128)S(1)}, f32[2,56,768]{2,1,0:T(8,128)S(1)}, u32[]{:S(2)}, u32[]{:S(2)}) collective-permute-start(f32[2,56,768]{2,1,0:T(8,128)S(1)} %copy-done.45), channel_id=1, source_target_pairs={{0,8},{1,9},{2,10},{3,11},{4,12},{5,13},{6,14},{7,15},{8,0},{9,1},... | collective-permute-start | bytes 1032200 | tf_op jit(solution)/shard_map/ppermute | solution.py:51
  765.8 20.0 %collective-permute-done.65 = f32[4,56,1280]{2,1,0:T(8,128)S(1)} collective-permute-done((f32[4,56,1280]{2,1,0:T(8,128)S(1)}, f32[4,56,1280]{2,1,0:T(8,128)S(1)}, u32[]{:S(2)}, u32[]{:S(2)}) %collective-permute-start.65) | collective-permute-done | bytes 1146912 | tf_op jit(solution)/shard_map/ppermute | solution.py:51
  798.6 11.8 %collective-permute-start.70 = (f32[56,1280]{1,0:T(8,128)S(1)}, f32[56,1280]{1,0:T(8,128)S(1)}, u32[]{:S(2)}, u32[]{:S(2)}) collective-permute-start(f32[56,1280]{1,0:T(8,128)S(1)} %get-tuple-element.381), channel_id=1, source_target_pairs={{0,8},{1,9},{2,10},{3,11},{4,12},{5,13},{6,14},{7,15},{8,0},{9,1},... | collective-permute-start | bytes 860168 | tf_op jit(solution)/shard_map/ppermute | solution.py:51
  810.4 40.6 %add_convert_fusion = bf16[4096,2048]{1,0:T(8,128)(2,1)} fusion(f32[4096,2048]{1,0:T(8,128)} %fusion.82, bf16[1792,4096]{1,0:T(8,128)(2,1)} %all-gather.11.cloned.1.call-done, bf16[1792,2048]{1,0:T(8,128)(2,1)} %copy-done.10), kind=kOutput, calls=%fused_computation.51 | convolution fusion | flops 30081548288 | bytes 72351744 | tf_op jit(solution)/shard_map/td,tv->dv/dot_general | solution.py:183
  (556 shorter events, 365.8 us)
Async XLA Ops:
  7.2 152.0 %all-gather.9.cloned.1.call-start = ((), (), s32[]{:S(2)}) async-start(), calls=%async_computation.2 | async-start | bytes 17301504 | tf_op jit(solution)/shard_map/all_gather | solution.py:82
  17.0 306.8 %all-gather.11.cloned.1.call-start = ((), (), s32[]{:S(2)}) async-start(), calls=%async_computation.3 | async-start | bytes 15138816 | tf_op jit(solution)/shard_map/all_gather | solution.py:82
  267.8 50.0 %collective-permute-start.19 = (bf16[4,2,64,768]{3,2,1,0:T(8,128)(2,1)}, bf16[4,2,64,768]{3,2,1,0:T(8,128)(2,1)}, u32[]{:S(2)}, u32[]{:S(2)}) collective-permute-start(bf16[4,2,64,768]{3,2,1,0:T(8,128)(2,1)} %get-tuple-element.348), channel_id=1, source_target_pairs={{0,5},{1,4},{2,7},{3,6},{4,1},{5,0},{6,3},{7,2},{8,13},{9,12},{10,... | collective-permute-start | bytes 2359304 | tf_op jit(solution)/shard_map/ppermute | solution.py:51
  386.8 52.6 %collective-permute-start.33 = (bf16[4,2,64,1280]{3,2,0,1:T(8,128)(2,1)S(1)}, bf16[4,2,64,1280]{3,2,0,1:T(8,128)(2,1)S(1)}, u32[]{:S(2)}, u32[]{:S(2)}) collective-permute-start(bf16[4,2,64,1280]{3,2,0,1:T(8,128)(2,1)S(1)} %bitcast.296), channel_id=1, source_target_pairs={{0,3},{1,2},{2,1},{3,0},{4,7},{5,6},{6,5},{7,4},{8,11},{9,10},{10,... | collective-permute-start | bytes 3932168 | tf_op jit(solution)/shard_map/ppermute | solution.py:51
  386.8 55.2 %collective-permute-start.34 = (bf16[4,2,64,1280]{3,2,0,1:T(8,128)(2,1)S(1)}, bf16[4,2,64,1280]{3,2,0,1:T(8,128)(2,1)S(1)}, u32[]{:S(2)}, u32[]{:S(2)}) collective-permute-start(bf16[4,2,64,1280]{3,2,0,1:T(8,128)(2,1)S(1)} %bitcast.294), channel_id=1, source_target_pairs={{0,1},{1,0},{2,3},{3,2},{4,5},{5,4},{6,7},{7,6},{8,9},{9,8},{10,11... | collective-permute-start | bytes 3932168 | tf_op jit(solution)/shard_map/ppermute | solution.py:51
  388.8 53.3 %collective-permute-start.29 = (bf16[4,2,64,1280]{3,2,0,1:T(8,128)(2,1)S(1)}, bf16[4,2,64,1280]{3,2,0,1:T(8,128)(2,1)S(1)}, u32[]{:S(2)}, u32[]{:S(2)}) collective-permute-start(bf16[4,2,64,1280]{3,2,0,1:T(8,128)(2,1)S(1)} %bitcast.297), channel_id=1, source_target_pairs={{0,4},{1,5},{2,6},{3,7},{4,0},{5,1},{6,2},{7,3},{8,12},{9,13},{10,... | collective-permute-start | bytes 3932168 | tf_op jit(solution)/shard_map/ppermute | solution.py:51
  395.4 51.4 %collective-permute-start.30 = (bf16[4,2,64,1280]{3,2,0,1:T(8,128)(2,1)S(1)}, bf16[4,2,64,1280]{3,2,0,1:T(8,128)(2,1)S(1)}, u32[]{:S(2)}, u32[]{:S(2)}) collective-permute-start(bf16[4,2,64,1280]{3,2,0,1:T(8,128)(2,1)S(1)} %bitcast.295), channel_id=1, source_target_pairs={{0,5},{1,4},{2,7},{3,6},{4,1},{5,0},{6,3},{7,2},{8,13},{9,12},{10,... | collective-permute-start | bytes 3932168 | tf_op jit(solution)/shard_map/ppermute | solution.py:51
  442.1 50.3 %collective-permute-start.27 = (f32[2,64,768]{2,1,0:T(8,128)S(1)}, f32[2,64,768]{2,1,0:T(8,128)S(1)}, u32[]{:S(2)}, u32[]{:S(2)}) collective-permute-start(f32[2,64,768]{2,1,0:T(8,128)S(1)} %copy-done.43), channel_id=1, source_target_pairs={{0,16},{1,17},{2,18},{3,19},{4,20},{5,21},{6,22},{7,23},{8,24},{9,... | collective-permute-start | bytes 1179656 | tf_op jit(solution)/shard_map/ppermute | solution.py:51
  442.2 53.1 %collective-permute-start.26 = (f32[2,64,768]{2,1,0:T(8,128)S(1)}, f32[2,64,768]{2,1,0:T(8,128)S(1)}, u32[]{:S(2)}, u32[]{:S(2)}) collective-permute-start(f32[2,64,768]{2,1,0:T(8,128)S(1)} %copy-done.40), channel_id=1, source_target_pairs={{0,8},{1,9},{2,10},{3,11},{4,12},{5,13},{6,14},{7,15},{8,0},{9,1},... | collective-permute-start | bytes 1179656 | tf_op jit(solution)/shard_map/ppermute | solution.py:51
  446.8 49.5 %collective-permute-start.38 = (f32[2,64,768]{2,1,0:T(8,128)S(1)}, f32[2,64,768]{2,1,0:T(8,128)S(1)}, u32[]{:S(2)}, u32[]{:S(2)}) collective-permute-start(f32[2,64,768]{2,1,0:T(8,128)S(1)} %copy-done.42), channel_id=1, source_target_pairs={{0,24},{1,25},{2,26},{3,27},{4,28},{5,29},{6,30},{7,31},{8,16},{9,... | collective-permute-start | bytes 1179656 | tf_op jit(solution)/shard_map/ppermute | solution.py:51
  448.3 60.9 %collective-permute-start.37 = (f32[2,64,768]{2,1,0:T(8,128)S(1)}, f32[2,64,768]{2,1,0:T(8,128)S(1)}, u32[]{:S(2)}, u32[]{:S(2)}) collective-permute-start(f32[2,64,768]{2,1,0:T(8,128)S(1)} %copy-done.41), channel_id=1, source_target_pairs={{0,16},{1,17},{2,18},{3,19},{4,20},{5,21},{6,22},{7,23},{8,24},{9,... | collective-permute-start | bytes 1179656 | tf_op jit(solution)/shard_map/ppermute | solution.py:51
  452.1 57.2 %collective-permute-start.36 = (f32[2,64,768]{2,1,0:T(8,128)S(1)}, f32[2,64,768]{2,1,0:T(8,128)S(1)}, u32[]{:S(2)}, u32[]{:S(2)}) collective-permute-start(f32[2,64,768]{2,1,0:T(8,128)S(1)} %get-tuple-element.345), channel_id=1, source_target_pairs={{0,8},{1,9},{2,10},{3,11},{4,12},{5,13},{6,14},{7,15},{8,0},{9,1},... | collective-permute-start | bytes 1179656 | tf_op jit(solution)/shard_map/ppermute | solution.py:51
  560.9 63.8 %collective-permute-start.45 = (bf16[4,2,56,1280]{3,2,0,1:T(8,128)(2,1)}, bf16[4,2,56,1280]{3,2,0,1:T(8,128)(2,1)}, u32[]{:S(2)}, u32[]{:S(2)}) collective-permute-start(bf16[4,2,56,1280]{3,2,0,1:T(8,128)(2,1)} %bitcast.268), channel_id=1, source_target_pairs={{0,3},{1,2},{2,1},{3,0},{4,7},{5,6},{6,5},{7,4},{8,11},{9,10},{10,... | collective-permute-start | bytes 3440648 | tf_op jit(solution)/shard_map/ppermute | solution.py:51
  560.9 64.7 %collective-permute-start.46 = (bf16[4,2,56,1280]{3,2,0,1:T(8,128)(2,1)}, bf16[4,2,56,1280]{3,2,0,1:T(8,128)(2,1)}, u32[]{:S(2)}, u32[]{:S(2)}) collective-permute-start(bf16[4,2,56,1280]{3,2,0,1:T(8,128)(2,1)} %bitcast.267), channel_id=1, source_target_pairs={{0,1},{1,0},{2,3},{3,2},{4,5},{5,4},{6,7},{7,6},{8,9},{9,8},{10,11... | collective-permute-start | bytes 3440648 | tf_op jit(solution)/shard_map/ppermute | solution.py:51
  579.1 96.8 %collective-permute-start.58 = (f32[64,1280]{1,0:T(8,128)}, f32[64,1280]{1,0:T(8,128)}, u32[]{:S(2)}, u32[]{:S(2)}) collective-permute-start(f32[64,1280]{1,0:T(8,128)} %get-tuple-element.376), channel_id=1, source_target_pairs={{0,16},{1,17},{2,18},{3,19},{4,20},{5,21},{6,22},{7,23},{8,24},{9,... | collective-permute-start | bytes 983048 | tf_op jit(solution)/shard_map/ppermute | solution.py:51
  586.6 91.0 %collective-permute-start.57 = (f32[64,1280]{1,0:T(8,128)}, f32[64,1280]{1,0:T(8,128)}, u32[]{:S(2)}, u32[]{:S(2)}) collective-permute-start(f32[64,1280]{1,0:T(8,128)} %get-tuple-element.377), channel_id=1, source_target_pairs={{0,8},{1,9},{2,10},{3,11},{4,12},{5,13},{6,14},{7,15},{8,0},{9,1},... | collective-permute-start | bytes 983048 | tf_op jit(solution)/shard_map/ppermute | solution.py:51
  601.9 66.6 %collective-permute-start.41 = (bf16[4,2,56,1280]{3,2,0,1:T(8,128)(2,1)}, bf16[4,2,56,1280]{3,2,0,1:T(8,128)(2,1)S(1)}, u32[]{:S(2)}, u32[]{:S(2)}) collective-permute-start(bf16[4,2,56,1280]{3,2,0,1:T(8,128)(2,1)} %bitcast.265), channel_id=1, source_target_pairs={{0,4},{1,5},{2,6},{3,7},{4,0},{5,1},{6,2},{7,3},{8,12},{9,13},{10,... | collective-permute-start | bytes 3440648 | tf_op jit(solution)/shard_map/ppermute | solution.py:51
  681.8 79.8 %collective-permute-start.68 = (f32[2,56,768]{2,1,0:T(8,128)}, f32[2,56,768]{2,1,0:T(8,128)S(1)}, u32[]{:S(2)}, u32[]{:S(2)}) collective-permute-start(f32[2,56,768]{2,1,0:T(8,128)} %get-tuple-element.359), channel_id=1, source_target_pairs={{0,24},{1,25},{2,26},{3,27},{4,28},{5,29},{6,30},{7,31},{8,16},{9,... | collective-permute-start | bytes 1032200 | tf_op jit(solution)/shard_map/ppermute | solution.py:51
  706.5 55.1 %collective-permute-start.67 = (f32[2,56,768]{2,1,0:T(8,128)}, f32[2,56,768]{2,1,0:T(8,128)S(1)}, u32[]{:S(2)}, u32[]{:S(2)}) collective-permute-start(f32[2,56,768]{2,1,0:T(8,128)} %get-tuple-element.360), channel_id=1, source_target_pairs={{0,16},{1,17},{2,18},{3,19},{4,20},{5,21},{6,22},{7,23},{8,24},{9,... | collective-permute-start | bytes 1032200 | tf_op jit(solution)/shard_map/ppermute | solution.py:51
  791.8 60.3 %collective-permute-start.74 = (f32[56,1280]{1,0:T(8,128)S(1)}, f32[56,1280]{1,0:T(8,128)S(1)}, u32[]{:S(2)}, u32[]{:S(2)}) collective-permute-start(f32[56,1280]{1,0:T(8,128)S(1)} %get-tuple-element.384), channel_id=1, source_target_pairs={{0,16},{1,17},{2,18},{3,19},{4,20},{5,21},{6,22},{7,23},{8,24},{9,... | collective-permute-start | bytes 860168 | tf_op jit(solution)/shard_map/ppermute | solution.py:51
  791.9 60.2 %collective-permute-start.73 = (f32[56,1280]{1,0:T(8,128)S(1)}, f32[56,1280]{1,0:T(8,128)S(1)}, u32[]{:S(2)}, u32[]{:S(2)}) collective-permute-start(f32[56,1280]{1,0:T(8,128)S(1)} %get-tuple-element.385), channel_id=1, source_target_pairs={{0,8},{1,9},{2,10},{3,11},{4,12},{5,13},{6,14},{7,15},{8,0},{9,1},... | collective-permute-start | bytes 860168 | tf_op jit(solution)/shard_map/ppermute | solution.py:51
  794.8 57.3 %collective-permute-start.72 = (f32[56,1280]{1,0:T(8,128)S(1)}, f32[56,1280]{1,0:T(8,128)S(1)}, u32[]{:S(2)}, u32[]{:S(2)}) collective-permute-start(f32[56,1280]{1,0:T(8,128)S(1)} %copy-done.54), channel_id=1, source_target_pairs={{0,24},{1,25},{2,26},{3,27},{4,28},{5,29},{6,30},{7,31},{8,16},{9,... | collective-permute-start | bytes 860168 | tf_op jit(solution)/shard_map/ppermute | solution.py:51
  796.4 55.7 %collective-permute-start.71 = (f32[56,1280]{1,0:T(8,128)S(1)}, f32[56,1280]{1,0:T(8,128)S(1)}, u32[]{:S(2)}, u32[]{:S(2)}) collective-permute-start(f32[56,1280]{1,0:T(8,128)S(1)} %get-tuple-element.380), channel_id=1, source_target_pairs={{0,16},{1,17},{2,18},{3,19},{4,20},{5,21},{6,22},{7,23},{8,24},{9,... | collective-permute-start | bytes 860168 | tf_op jit(solution)/shard_map/ppermute | solution.py:51
  798.6 53.5 %collective-permute-start.70 = (f32[56,1280]{1,0:T(8,128)S(1)}, f32[56,1280]{1,0:T(8,128)S(1)}, u32[]{:S(2)}, u32[]{:S(2)}) collective-permute-start(f32[56,1280]{1,0:T(8,128)S(1)} %get-tuple-element.381), channel_id=1, source_target_pairs={{0,8},{1,9},{2,10},{3,11},{4,12},{5,13},{6,14},{7,15},{8,0},{9,1},... | collective-permute-start | bytes 860168 | tf_op jit(solution)/shard_map/ppermute | solution.py:51
  (138 other events, 3131.8 us)
Sparse Core Ops, SparseCore 0:
  17.1 129.7 all-gather.8
  149.7 106.0 all-gather.10
where the time goes:
time: 935 us; the launch traced here: 925 us
  waiting for transfers between devices  306 us (33%)
  matrix products  256 us (27%)
  starting transfers between devices  145 us (16%)
  other arithmetic  89.8 us (10%)
  local copies, waits for them, and re-layouts  53.9 us (6%)
  blocking collectives  43.8 us (5%)
  between operations  30.2 us (3%)
    ppermute x86, waiting for transfers between devices, swap(): return lax.ppermute(a, 'tp', [(i, i ^ flip) for i in range(n)])  306 us
    ppermute x86, starting transfers between devices, swap(): return lax.ppermute(a, 'tp', [(i, i ^ flip) for i in range(n)])  145 us
    dot_general x8, matrix products, hidden_grad(): jnp.einsum('tv,dv->td', dl, w_part, preferred_element_type=f32)  91.6 us
    dot_general x2, matrix products, head_grad(): term = jnp.einsum('td,tv->dv', hn[c], dl, preferred_element_type=f32)  83.1 us
    dot_general x2, matrix products, forward(): lg = jnp.einsum('td,dv->tv', hn[c], w_head, preferred_element_type=f32)  81.3 us
    unnamed x1, blocking collectives  43.8 us
  transfers between devices with their start and end apart: 88, of which 43 were waited for; matrix products, arithmetic and copies ran while one was open for 35% of the time, Pallas kernels for 0%

commit v1 on v0

--- a/solution.py
+++ b/solution.py
@@ -4,8 +4,8 @@
 from jax.sharding import PartitionSpec as P
 
 NORM_EPS = 1e-6
-STAGES = ((1, 64), (2, 56), (4, 40), (8, 32), (16, 24))
-ROWS = (64, 56)
+STAGES = ((1, 72), (2, 56), (4, 40), (8, 32), (16, 24))
+ROWS = (56, 64)
 UNITS = ((('y', 'z', 'x'), 6), (('x', 'z', 'y'), 6), (('x', 'y', 'z'), 10), (('y', 'x', 'z'), 10))
 
 
@@ -53,6 +53,15 @@
     def at(a, axis, i):
         return lax.dynamic_index_in_dim(a, i, axis, keepdims=False)
 
+    def in_order(rows):
+        return jnp.take(rows, jnp.arange(n, dtype=jnp.int32) ^ lax.axis_index('tp'), axis=0, mode='clip')
+
+    def gather_small(a):
+        rows = a[None]
+        for bit in bits:
+            rows = jnp.concatenate([rows, swap(rows, bit)])
+        return in_order(rows)
+
     def after(values, dep):
         return lax.optimization_barrier((values, dep))[0]
 
@@ -72,7 +81,8 @@
         order = jnp.sum(jnp.where(chosen, all_slots[None, :], 0), axis=1)
         packed_lab = jnp.sum(jnp.where(chosen, labels.reshape(n_rows)[None, :] + 1, 0), axis=1) - 1
         packed = jnp.take(hidden.reshape(n_rows, model_width), order, axis=0, mode='clip')
-        count = jnp.maximum(jnp.sum(mask) - ROWS[0], 0)
+        kept = jnp.sum(mask)
+        count = jnp.maximum(kept - ROWS[0], 0)
         n_rest = n_rows - ROWS[0]
         slot = jnp.arange(n_rest, dtype=i32)
 
@@ -84,32 +94,36 @@
         hn, vjps = [None, None], [None, None]
         hn[0], vjps[0], sent = normed(packed[:ROWS[0]])
         rows, lab = after((packed[ROWS[0]:], packed_lab[ROWS[0]:]), sent)
+        known = jnp.concatenate([packed_lab[:ROWS[0]], jnp.full((128 - ROWS[0],), kept, i32)])
         fits = jnp.bool_(True)
         moves = []
         for bit, cap in STAGES:
             start = jnp.maximum(count - cap, 0)
-            ints = jnp.concatenate([lax.dynamic_slice_in_dim(lab, start, cap), jnp.full((128,), count, i32)])
+            ints = jnp.concatenate([known, jnp.full((128,), count, i32), lax.dynamic_slice_in_dim(lab, start, cap)])
             got_rows = swap(lax.dynamic_slice_in_dim(rows, start, cap), bit)
             got_ints = swap(ints, bit)
-            other = got_ints[cap]
+            size = known.shape[0]
+            known = jnp.concatenate([known, got_ints[:size]])
+            other, got_lab = got_ints[size], got_ints[size + 128:]
             upper = (me & bit) // bit
             target = (count + other + 1 - upper) >> 1
             fits = fits & (jnp.abs(target - count) <= cap)
             first = count + other - target - jnp.maximum(other - cap, 0)
             src = jnp.where(slot < count, slot, n_rest + jnp.clip(first + slot - count, 0, cap - 1))
             rows = jnp.take(jnp.concatenate([rows, got_rows]), src, axis=0, mode='clip')
-            lab = jnp.take(jnp.concatenate([lab, got_ints[:cap]]), src, axis=0, mode='clip')
+            lab = jnp.take(jnp.concatenate([lab, got_lab]), src, axis=0, mode='clip')
             moves.append((bit, cap, count, other, target))
             count = target
+        known = in_order(known.reshape(n, 128))
+        label_all = [known[:, :ROWS[0]].reshape(-1)]
+        kept_count = jnp.sum(known[:, ROWS[0]]).astype(f32)
         fits = fits & (count <= ROWS[1])
         hn[1], vjps[1], _ = normed(rows[:ROWS[1]])
         lab = jnp.where(slot < count, lab, -1)[:ROWS[1]]
-        rows_all = sum(ROWS)
-        known = lax.all_gather(jnp.concatenate([packed_lab[:ROWS[0]], lab, jnp.full((128,), fits.astype(i32))]), 'tp', axis=0, tiled=False)
-        all_fit = jnp.min(known[:, rows_all]) == 1
-        label_all = [k.reshape(-1) for k in jnp.split(known[:, :rows_all], [ROWS[0]], axis=1)]
+        known = gather_small(jnp.concatenate([lab, jnp.full((128 - ROWS[1],), fits.astype(i32))]))
+        label_all.append(known[:, :ROWS[1]].reshape(-1))
+        all_fit = jnp.min(known[:, ROWS[1]]) == 1
         weight = [(lb >= 0).astype(f32) for lb in label_all]
-        kept_count = sum(jnp.sum(w) for w in weight)
         cols = lax.broadcasted_iota(i32, (1, v_loc), 1) + me * v_loc
 
         def forward(c):
@@ -219,16 +233,15 @@
         d_x, d_gain = (early[0], late[0].astype(jnp.bfloat16)), early[1] + late[1]
         loss = sum(jnp.sum(weight[c] * (log_norm[c] - label_logit[c])) for c in range(2))
         mean_loss = loss / kept_count
-        for bit in bits:
+
+        room = n_rest - ROWS[1] + max(cap for _, cap in STAGES)
+        back = jnp.concatenate([*d_x, jnp.zeros((room, model_width), jnp.bfloat16)])
+        for bit, cap, count, other, target in reversed(moves):
+            got = swap(lax.dynamic_slice_in_dim(back, ROWS[0] + count, cap), bit)
             d_gain = d_gain + swap(d_gain, bit)
-
-        back = jnp.concatenate([d_x[1], jnp.zeros((n_rest - ROWS[1], model_width), jnp.bfloat16)])
-        for bit, cap, count, other, target in reversed(moves):
-            got = swap(lax.dynamic_slice_in_dim(back, jnp.minimum(count, n_rest - cap), cap), bit)
-            first = jnp.maximum(other - (n_rest - cap), 0)
-            src = jnp.where(slot < target, slot, n_rest + jnp.clip(first + slot - target, 0, cap - 1))
-            back = jnp.take(jnp.concatenate([back, got]), src, axis=0, mode='clip')
-        back = jnp.take(jnp.concatenate([d_x[0], back]), pos, axis=0, mode='clip')
+            back = lax.dynamic_update_slice_in_dim(back, got, ROWS[0] + target, 0)
+            back, d_gain = lax.optimization_barrier((back, d_gain))
+        back = jnp.take(back, pos, axis=0, mode='clip')
         d_hidden = jnp.where(mask[:, None] == 1, back, jnp.zeros((), jnp.bfloat16)).reshape(hidden.shape)
 
         def every_token(_):

time: 935 us -> 856 us (0.916)
  blocking collectives: 43.8 us -> 0 us
  starting transfers between devices: 145 us -> 130 us
  waiting for transfers between devices: 306 us -> 293 us
    unnamed x1 -> x0, blocking collectives: 43.8 us -> none
    ppermute x86 -> x91, waiting for transfers between devices: 306 us -> 266 us  [swap(): return lax.ppermute(a, 'tp', [(i, i ^ flip) for i in range(n)])]
    all_gather x2, waiting for transfers between devices: 0.01 us -> 27.4 us  [normed(): return (lax.all_gather(out, 'tp', axis=0, tiled=True), vjp, out)]
    ppermute x86 -> x91, starting transfers between devices: 145 us -> 130 us  [swap(): return lax.ppermute(a, 'tp', [(i, i ^ flip) for i in range(n)])]
    dynamic_update_slice x0 -> x5, local copies, waits for them, and re-layouts: none -> 9.81 us  [device_step(): back = lax.dynamic_update_slice_in_dim(back, got, ROWS[0] + target, 0)]
  transfers between devices with their start and end apart: 88 -> 93, of which waited for: 43 -> 38; matrix products, arithmetic and copies ran while one was open for 35% -> 43% of each run, Pallas kernels for 0% -> 0%
where the time goes in v1:
time: 856 us; the launch traced here: 851 us
  waiting for transfers between devices  293 us (34%)
  matrix products  257 us (30%)
  starting transfers between devices  130 us (15%)
  other arithmetic  88.1 us (10%)
  local copies, waits for them, and re-layouts  54.4 us (6%)
  between operations  27.6 us (3%)
    ppermute x91, waiting for transfers between devices, swap(): return lax.ppermute(a, 'tp', [(i, i ^ flip) for i in range(n)])  266 us
    ppermute x91, starting transfers between devices, swap(): return lax.ppermute(a, 'tp', [(i, i ^ flip) for i in range(n)])  130 us
    dot_general x8, matrix products, hidden_grad(): jnp.einsum('tv,dv->td', dl, w_part, preferred_element_type=f32)  92.1 us
    dot_general x2, matrix products, head_grad(): term = jnp.einsum('td,tv->dv', hn[c], dl, preferred_element_type=f32)  83.2 us
    dot_general x2, matrix products, forward(): lg = jnp.einsum('td,dv->tv', hn[c], w_head, preferred_element_type=f32)  81.8 us
    all_gather x2, waiting for transfers between devices, normed(): return (lax.all_gather(out, 'tp', axis=0, tiled=True), vjp, out)  27.4 us
    reduce_sum x2, other arithmetic, forward(): row_sum = jnp.sum(jnp.exp(lg - row_max[:, None]), axis=-1)  17.5 us
    add x8, other arithmetic, second(): sum((at(t, axis, i).astype(f32) for t in terms))  17.3 us
  transfers between devices with their start and end apart: 93, of which 38 were waited for; matrix products, arithmetic and copies ran while one was open for 43% of the time, Pallas kernels for 0%

profile of v1, /device:TPU:0, one launch (start us, length us, event | category | flops | bytes accessed | tf_op | source)
XLA Modules:
  0.0 851.3 jit_solution(4448213074692702058)
XLA Ops:
  29.1 12.5 %collective-permute-done.1 = s32[440]{0:T(512)S(1)} collective-permute-done((s32[440]{0:T(512)S(1)}, s32[440]{0:T(512)S(1)}, u32[]{:S(2)}, u32[]{:S(2)}) %collective-permute-start.1) | collective-permute-done | bytes 1792 | tf_op jit(solution)/shard_map/ppermute | solution.py:51
  84.9 15.8 %collective-permute-done.19 = bf16[24,4096]{1,0:T(8,128)(2,1)S(1)} collective-permute-done((bf16[24,4096]{1,0:T(8,128)(2,1)S(1)}, bf16[24,4096]{1,0:T(8,128)(2,1)S(1)}, u32[]{:S(2)}, u32[]{:S(2)}) %collective-permute-start.19) | collective-permute-done | bytes 196640 | tf_op jit(solution)/shard_map/ppermute | solution.py:51
  107.7 27.4 %all-gather.8.cloned.1.call-done = bf16[1792,4096]{1,0:T(8,128)(2,1)} async-done(((bf16[56,4096]{1,0:T(8,128)(2,1)}), bf16[1792,4096]{1,0:T(8,128)(2,1)}) %all-gather.8.cloned.1.call-update) | async-done | bytes 14680080 | tf_op jit(solution)/shard_map/all_gather | solution.py:92
  135.1 38.6 %fusion.70 = f32[1792,2048]{1,0:T(8,128)} fusion(bf16[1792,4096]{1,0:T(8,128)(2,1)} %all-gather.8.cloned.1.call-done, bf16[4096,2048]{1,0:T(8,128)(2,1)} %param.11), kind=kOutput, calls=%fused_computation.369 | convolution fusion | flops 30064771072 | bytes 46137344 | tf_op jit(solution)/shard_map/td,dv->tv/dot_general | solution.py:130
  218.8 10.6 %convolution_convert_fusion.8 = bf16[1792,768]{1,0:T(8,128)(2,1)S(1)} fusion(bf16[1792,2048]{1,0:T(8,128)(2,1)S(1)} %fusion.25, bf16[4096,2048]{1,0:T(8,128)(2,1)} %param.11), kind=kOutput, calls=%fused_computation.74 | convolution fusion | flops 5638520832 | bytes 13238272 | tf_op jit(solution)/shard_map/tv,dv->td/dot_general | solution.py:191
  241.4 12.6 %convolution_convert_fusion.4 = bf16[1792,1280]{1,0:T(8,128)(2,1)S(1)} fusion(bf16[1792,2048]{1,0:T(8,128)(2,1)S(1)} %fusion.25, bf16[4096,2048]{1,0:T(8,128)(2,1)} %param.11), kind=kOutput, calls=%fused_computation.66 | convolution fusion | flops 9397534720 | bytes 17170432 | tf_op jit(solution)/shard_map/tv,dv->td/dot_general | solution.py:191
  258.6 12.5 %convolution_convert_fusion.3 = bf16[1792,1280]{1,0:T(8,128)(2,1)S(1)} fusion(bf16[1792,2048]{1,0:T(8,128)(2,1)S(1)} %fusion.25, bf16[4096,2048]{1,0:T(8,128)(2,1)} %param.11), kind=kOutput, calls=%fused_computation.65 | convolution fusion | flops 9397534720 | bytes 17170432 | tf_op jit(solution)/shard_map/tv,dv->td/dot_general | solution.py:191
  280.5 43.2 %fusion.71 = f32[2048,2048]{1,0:T(8,128)} fusion(bf16[2048,4096]{1,0:T(8,128)(2,1)} %all-gather.10.cloned.1.call-done, bf16[4096,2048]{1,0:T(8,128)(2,1)} %param.11), kind=kOutput, calls=%fused_computation.370 | convolution fusion | flops 34359738368 | bytes 50331648 | tf_op jit(solution)/shard_map/td,dv->tv/dot_general | solution.py:130
  330.3 9.7 %exponential_reduce_fusion.1 = (f32[2048]{0:T(1024)S(1)}, f32[2048]{0:T(1024)S(1)}) fusion(f32[2048,2048]{1,0:T(8,128)} %fusion.71, f32[2048]{0:T(1024)S(1)} %reduce_max.28, s32[2048]{0:T(1024)S(1)} %eq.100, s32[2048]{0:T(1024)S(1)} %iota_add_fusion.1), kind=kLoop, calls=%fused_computation.57 | loop fusion | flops 20967424 | bytes 16818176 | tf_op jit(solution)/shard_map/reduce_sum | solution.py:133
  347.7 20.7 %collective-permute-done.34 = bf16[4,2,56,1280]{3,2,0,1:T(8,128)(2,1)S(1)} collective-permute-done((bf16[4,2,56,1280]{3,2,0,1:T(8,128)(2,1)S(1)}, bf16[4,2,56,1280]{3,2,0,1:T(8,128)(2,1)S(1)}, u32[]{:S(2)}, u32[]{:S(2)}) %collective-permute-start.34) | collective-permute-done | bytes 1146912 | tf_op jit(solution)/shard_map/ppermute | solution.py:51
  369.0 22.9 %collective-permute-done.35 = bf16[4,2,56,1280]{3,2,0,1:T(8,128)(2,1)S(1)} collective-permute-done((bf16[4,2,56,1280]{3,2,0,1:T(8,128)(2,1)S(1)}, bf16[4,2,56,1280]{3,2,0,1:T(8,128)(2,1)S(1)}, u32[]{:S(2)}, u32[]{:S(2)}) %collective-permute-start.35) | collective-permute-done | bytes 1146912 | tf_op jit(solution)/shard_map/ppermute | solution.py:51
  397.3 11.5 %collective-permute-done.32 = f32[2,56,768]{2,1,0:T(8,128)S(1)} collective-permute-done((f32[2,56,768]{2,1,0:T(8,128)S(1)}, f32[2,56,768]{2,1,0:T(8,128)S(1)}, u32[]{:S(2)}, u32[]{:S(2)}) %collective-permute-start.32) | collective-permute-done | bytes 344096 | tf_op jit(solution)/shard_map/ppermute | solution.py:51
  437.2 11.2 %convolution_convert_fusion.6 = bf16[2048,768]{1,0:T(8,128)(2,1)S(1)} fusion(bf16[2048,2048]{1,0:T(8,128)(2,1)S(1)} %fusion.21, bf16[4096,2048]{1,0:T(8,128)(2,1)} %param.11), kind=kOutput, calls=%fused_computation.72 | convolution fusion | flops 6444023808 | bytes 14680064 | tf_op jit(solution)/shard_map/tv,dv->td/dot_general | solution.py:191
  466.9 13.7 %convolution_convert_fusion.2 = bf16[2048,1280]{1,0:T(8,128)(2,1)S(1)} fusion(bf16[2048,2048]{1,0:T(8,128)(2,1)S(1)} %fusion.21, bf16[4096,2048]{1,0:T(8,128)(2,1)} %param.11), kind=kOutput, calls=%fused_computation.64 | convolution fusion | flops 10740039680 | bytes 18874368 | tf_op jit(solution)/shard_map/tv,dv->td/dot_general | solution.py:191
  483.4 13.9 %convolution_convert_fusion.1 = bf16[2048,1280]{1,0:T(8,128)(2,1)S(1)} fusion(bf16[2048,2048]{1,0:T(8,128)(2,1)S(1)} %fusion.21, bf16[4096,2048]{1,0:T(8,128)(2,1)} %param.11), kind=kOutput, calls=%fused_computation.63 | convolution fusion | flops 10740039680 | bytes 18874368 | tf_op jit(solution)/shard_map/tv,dv->td/dot_general | solution.py:191
  506.6 23.7 %collective-permute-done.49 = bf16[4,2,64,1280]{3,2,0,1:T(8,128)(2,1)} collective-permute-done((bf16[4,2,64,1280]{3,2,0,1:T(8,128)(2,1)S(1)}, bf16[4,2,64,1280]{3,2,0,1:T(8,128)(2,1)}, u32[]{:S(2)}, u32[]{:S(2)}) %collective-permute-start.49) | collective-permute-done | bytes 1310752 | tf_op jit(solution)/shard_map/ppermute | solution.py:51
  530.2 37.7 %fusion.72 = f32[4096,2048]{1,0:T(8,128)} fusion(bf16[1792,4096]{1,0:T(8,128)(2,1)} %all-gather.8.cloned.1.call-done, bf16[1792,2048]{1,0:T(8,128)(2,1)S(1)} %bitcast.267), kind=kOutput, calls=%fused_computation.371 | convolution fusion | flops 30064771072 | bytes 55574528 | tf_op jit(solution)/shard_map/td,tv->dv/dot_general | solution.py:197
  582.4 19.7 %collective-permute-done.63 = f32[56,1280]{1,0:T(8,128)S(1)} collective-permute-done((f32[56,1280]{1,0:T(8,128)}, f32[56,1280]{1,0:T(8,128)S(1)}, u32[]{:S(2)}, u32[]{:S(2)}) %collective-permute-start.63) | collective-permute-done | bytes 286752 | tf_op jit(solution)/shard_map/ppermute | solution.py:51
  608.7 20.3 %collective-permute-done.60 = f32[56,1280]{1,0:T(8,128)S(1)} collective-permute-done((f32[56,1280]{1,0:T(8,128)S(1)}, f32[56,1280]{1,0:T(8,128)S(1)}, u32[]{:S(2)}, u32[]{:S(2)}) %collective-permute-start.60) | collective-permute-done | bytes 286752 | tf_op jit(solution)/shard_map/ppermute | solution.py:51
  642.9 20.8 %collective-permute-start.72 = (f32[2,64,768]{2,1,0:T(8,128)S(1)}, f32[2,64,768]{2,1,0:T(8,128)S(1)}, u32[]{:S(2)}, u32[]{:S(2)}) collective-permute-start(f32[2,64,768]{2,1,0:T(8,128)S(1)} %copy-done.31), channel_id=1, source_target_pairs={{0,16},{1,17},{2,18},{3,19},{4,20},{5,21},{6,22},{7,23},{8,24},{9,... | collective-permute-start | bytes 1179656 | tf_op jit(solution)/shard_map/ppermute | solution.py:51
  663.7 15.8 %collective-permute-done.66 = f32[2,64,768]{2,1,0:T(8,128)S(1)} collective-permute-done((f32[2,64,768]{2,1,0:T(8,128)S(1)}, f32[2,64,768]{2,1,0:T(8,128)S(1)}, u32[]{:S(2)}, u32[]{:S(2)}) %collective-permute-start.66) | collective-permute-done | bytes 393248 | tf_op jit(solution)/shard_map/ppermute | solution.py:51
  697.6 11.9 %collective-permute-done.69 = f32[4,64,1280]{2,1,0:T(8,128)S(1)} collective-permute-done((f32[4,64,1280]{2,1,0:T(8,128)S(1)}, f32[4,64,1280]{2,1,0:T(8,128)S(1)}, u32[]{:S(2)}, u32[]{:S(2)}) %collective-permute-start.69) | collective-permute-done | bytes 1310752 | tf_op jit(solution)/shard_map/ppermute | solution.py:51
  723.2 14.6 %collective-permute-start.75 = (f32[64,1280]{1,0:T(8,128)S(1)}, f32[64,1280]{1,0:T(8,128)}, u32[]{:S(2)}, u32[]{:S(2)}) collective-permute-start(f32[64,1280]{1,0:T(8,128)S(1)} %get-tuple-element.389), channel_id=1, source_target_pairs={{0,8},{1,9},{2,10},{3,11},{4,12},{5,13},{6,14},{7,15},{8,0},{9,1},... | collective-permute-start | bytes 983048 | tf_op jit(solution)/shard_map/ppermute | solution.py:51
  737.7 45.5 %add_convert_fusion = bf16[4096,2048]{1,0:T(8,128)(2,1)} fusion(f32[4096,2048]{1,0:T(8,128)} %fusion.72, bf16[2048,4096]{1,0:T(8,128)(2,1)} %all-gather.10.cloned.1.call-done, bf16[2048,2048]{1,0:T(8,128)(2,1)} %copy-done.7), kind=kOutput, calls=%fused_computation.48 | convolution fusion | flops 34376515584 | bytes 75497472 | tf_op jit(solution)/shard_map/td,tv->dv/dot_general | solution.py:197
  (595 shorter events, 336.9 us)
Async XLA Ops:
  7.2 128.0 %all-gather.8.cloned.1.call-start = ((), (), s32[]{:S(2)}) async-start(), calls=%async_computation.2 | async-start | bytes 15138816 | tf_op jit(solution)/shard_map/all_gather | solution.py:92
  15.6 264.9 %all-gather.10.cloned.1.call-start = ((), (), s32[]{:S(2)}) async-start(), calls=%async_computation.3 | async-start | bytes 17301504 | tf_op jit(solution)/shard_map/all_gather | solution.py:92
  107.6 80.3 %collective-permute-start.5 = (s32[1,128]{1,0:T(1,128)S(1)}, s32[1,128]{1,0:T(1,128)S(1)}, u32[]{:S(2)}, u32[]{:S(2)}) collective-permute-start(s32[1,128]{1,0:T(1,128)S(1)} %select_bitcast_fusion), channel_id=1, source_target_pairs={{0,1},{1,0},{2,3},{3,2},{4,5},{5,4},{6,7},{7,6},{8,9},{9,8},{10,11... | collective-permute-start | bytes 1544 | tf_op jit(solution)/shard_map/ppermute | solution.py:51
  274.8 67.2 %collective-permute-start.37 = (bf16[4,2,56,1280]{3,2,0,1:T(8,128)(2,1)}, bf16[4,2,56,1280]{3,2,0,1:T(8,128)(2,1)}, u32[]{:S(2)}, u32[]{:S(2)}) collective-permute-start(bf16[4,2,56,1280]{3,2,0,1:T(8,128)(2,1)} %bitcast.259), channel_id=1, source_target_pairs={{0,2},{1,3},{2,0},{3,1},{4,6},{5,7},{6,4},{7,5},{8,10},{9,11},{10,... | collective-permute-start | bytes 3440648 | tf_op jit(solution)/shard_map/ppermute | solution.py:51
  275.8 66.6 %collective-permute-start.38 = (bf16[4,2,56,1280]{3,2,0,1:T(8,128)(2,1)}, bf16[4,2,56,1280]{3,2,0,1:T(8,128)(2,1)}, u32[]{:S(2)}, u32[]{:S(2)}) collective-permute-start(bf16[4,2,56,1280]{3,2,0,1:T(8,128)(2,1)} %bitcast.258), channel_id=1, source_target_pairs={{0,3},{1,2},{2,1},{3,0},{4,7},{5,6},{6,5},{7,4},{8,11},{9,10},{10,... | collective-permute-start | bytes 3440648 | tf_op jit(solution)/shard_map/ppermute | solution.py:51
  277.1 65.8 %collective-permute-start.39 = (bf16[4,2,56,1280]{3,2,0,1:T(8,128)(2,1)}, bf16[4,2,56,1280]{3,2,0,1:T(8,128)(2,1)}, u32[]{:S(2)}, u32[]{:S(2)}) collective-permute-start(bf16[4,2,56,1280]{3,2,0,1:T(8,128)(2,1)} %bitcast.257), channel_id=1, source_target_pairs={{0,1},{1,0},{2,3},{3,2},{4,5},{5,4},{6,7},{7,6},{8,9},{9,8},{10,11... | collective-permute-start | bytes 3440648 | tf_op jit(solution)/shard_map/ppermute | solution.py:51
  342.0 49.9 %collective-permute-start.35 = (bf16[4,2,56,1280]{3,2,0,1:T(8,128)(2,1)S(1)}, bf16[4,2,56,1280]{3,2,0,1:T(8,128)(2,1)S(1)}, u32[]{:S(2)}, u32[]{:S(2)}) collective-permute-start(bf16[4,2,56,1280]{3,2,0,1:T(8,128)(2,1)S(1)} %bitcast.292), channel_id=1, source_target_pairs={{0,5},{1,4},{2,7},{3,6},{4,1},{5,0},{6,3},{7,2},{8,13},{9,12},{10,... | collective-permute-start | bytes 3440648 | tf_op jit(solution)/shard_map/ppermute | solution.py:51
  342.4 49.4 %collective-permute-start.36 = (bf16[4,2,56,1280]{3,2,0,1:T(8,128)(2,1)S(1)}, bf16[4,2,56,1280]{3,2,0,1:T(8,128)(2,1)S(1)}, u32[]{:S(2)}, u32[]{:S(2)}) collective-permute-start(bf16[4,2,56,1280]{3,2,0,1:T(8,128)(2,1)S(1)} %bitcast.291), channel_id=1, source_target_pairs={{0,1},{1,0},{2,3},{3,2},{4,5},{5,4},{6,7},{7,6},{8,9},{9,8},{10,11... | collective-permute-start | bytes 3440648 | tf_op jit(solution)/shard_map/ppermute | solution.py:51
  342.9 70.6 %collective-permute-start.43 = (f32[2,56,768]{2,1,0:T(8,128)S(1)}, f32[2,56,768]{2,1,0:T(8,128)S(1)}, u32[]{:S(2)}, u32[]{:S(2)}) collective-permute-start(f32[2,56,768]{2,1,0:T(8,128)S(1)} %copy-done.37), channel_id=1, source_target_pairs={{0,24},{1,25},{2,26},{3,27},{4,28},{5,29},{6,30},{7,31},{8,16},{9,... | collective-permute-start | bytes 1032200 | tf_op jit(solution)/shard_map/ppermute | solution.py:51
  409.8 52.9 %collective-permute-start.45 = (f32[4,56,1280]{2,1,0:T(8,128)S(1)}, f32[4,56,1280]{2,1,0:T(8,128)S(1)}, u32[]{:S(2)}, u32[]{:S(2)}) collective-permute-start(f32[4,56,1280]{2,1,0:T(8,128)S(1)} %get-tuple-element.343), channel_id=1, source_target_pairs={{0,4},{1,5},{2,6},{3,7},{4,0},{5,1},{6,2},{7,3},{8,12},{9,13},{10,... | collective-permute-start | bytes 3440648 | tf_op jit(solution)/shard_map/ppermute | solution.py:51
  413.6 50.2 %collective-permute-start.44 = (f32[4,56,1280]{2,1,0:T(8,128)S(1)}, f32[4,56,1280]{2,1,0:T(8,128)S(1)}, u32[]{:S(2)}, u32[]{:S(2)}) collective-permute-start(f32[4,56,1280]{2,1,0:T(8,128)S(1)} %get-tuple-element.345), channel_id=1, source_target_pairs={{0,2},{1,3},{2,0},{3,1},{4,6},{5,7},{6,4},{7,5},{8,10},{9,11},{10,... | collective-permute-start | bytes 3440648 | tf_op jit(solution)/shard_map/ppermute | solution.py:51
  498.4 69.6 %collective-permute-start.50 = (bf16[4,2,64,1280]{3,2,0,1:T(8,128)(2,1)S(1)}, bf16[4,2,64,1280]{3,2,0,1:T(8,128)(2,1)}, u32[]{:S(2)}, u32[]{:S(2)}) collective-permute-start(bf16[4,2,64,1280]{3,2,0,1:T(8,128)(2,1)S(1)} %bitcast.287), channel_id=1, source_target_pairs={{0,3},{1,2},{2,1},{3,0},{4,7},{5,6},{6,5},{7,4},{8,11},{9,10},{10,... | collective-permute-start | bytes 3932168 | tf_op jit(solution)/shard_map/ppermute | solution.py:51
  501.5 69.0 %collective-permute-start.51 = (bf16[4,2,64,1280]{3,2,0,1:T(8,128)(2,1)S(1)}, bf16[4,2,64,1280]{3,2,0,1:T(8,128)(2,1)}, u32[]{:S(2)}, u32[]{:S(2)}) collective-permute-start(bf16[4,2,64,1280]{3,2,0,1:T(8,128)(2,1)S(1)} %bitcast.285), channel_id=1, source_target_pairs={{0,1},{1,0},{2,3},{3,2},{4,5},{5,4},{6,7},{7,6},{8,9},{9,8},{10,11... | collective-permute-start | bytes 3932168 | tf_op jit(solution)/shard_map/ppermute | solution.py:51
  501.8 68.8 %collective-permute-start.46 = (bf16[4,2,64,1280]{3,2,0,1:T(8,128)(2,1)S(1)}, bf16[4,2,64,1280]{3,2,0,1:T(8,128)(2,1)S(1)}, u32[]{:S(2)}, u32[]{:S(2)}) collective-permute-start(bf16[4,2,64,1280]{3,2,0,1:T(8,128)(2,1)S(1)} %bitcast.290), channel_id=1, source_target_pairs={{0,4},{1,5},{2,6},{3,7},{4,0},{5,1},{6,2},{7,3},{8,12},{9,13},{10,... | collective-permute-start | bytes 3932168 | tf_op jit(solution)/shard_map/ppermute | solution.py:51
  503.6 71.6 %collective-permute-start.47 = (bf16[4,2,64,1280]{3,2,0,1:T(8,128)(2,1)S(1)}, bf16[4,2,64,1280]{3,2,0,1:T(8,128)(2,1)S(1)}, u32[]{:S(2)}, u32[]{:S(2)}) collective-permute-start(bf16[4,2,64,1280]{3,2,0,1:T(8,128)(2,1)S(1)} %bitcast.288), channel_id=1, source_target_pairs={{0,5},{1,4},{2,7},{3,6},{4,1},{5,0},{6,3},{7,2},{8,13},{9,12},{10,... | collective-permute-start | bytes 3932168 | tf_op jit(solution)/shard_map/ppermute | solution.py:51
  575.2 55.7 %collective-permute-start.58 = (f32[56,768]{1,0:T(8,128)S(1)}, f32[56,768]{1,0:T(8,128)S(1)}, u32[]{:S(2)}, u32[]{:S(2)}) collective-permute-start(f32[56,768]{1,0:T(8,128)S(1)} %copy-done.51), channel_id=1, source_target_pairs={{0,4},{1,5},{2,6},{3,7},{4,0},{5,1},{6,2},{7,3},{8,12},{9,13},{10,... | collective-permute-start | bytes 516104 | tf_op jit(solution)/shard_map/ppermute | solution.py:51
  576.5 56.9 %collective-permute-start.40 = (f32[56,768]{1,0:T(8,128)S(1)}, f32[56,768]{1,0:T(8,128)S(1)}, u32[]{:S(2)}, u32[]{:S(2)}) collective-permute-start(f32[56,768]{1,0:T(8,128)S(1)} %copy-done.50), channel_id=1, source_target_pairs={{0,2},{1,3},{2,0},{3,1},{4,6},{5,7},{6,4},{7,5},{8,10},{9,11},{10,... | collective-permute-start | bytes 516104 | tf_op jit(solution)/shard_map/ppermute | solution.py:51
  606.7 74.5 %collective-permute-start.73 = (f32[2,64,768]{2,1,0:T(8,128)S(1)}, f32[2,64,768]{2,1,0:T(8,128)S(1)}, u32[]{:S(2)}, u32[]{:S(2)}) collective-permute-start(f32[2,64,768]{2,1,0:T(8,128)S(1)} %copy-done.32), channel_id=1, source_target_pairs={{0,24},{1,25},{2,26},{3,27},{4,28},{5,29},{6,30},{7,31},{8,16},{9,... | collective-permute-start | bytes 1179656 | tf_op jit(solution)/shard_map/ppermute | solution.py:51
  633.4 63.3 %collective-permute-start.70 = (f32[4,64,1280]{2,1,0:T(8,128)S(1)}, f32[4,64,1280]{2,1,0:T(8,128)S(1)}, u32[]{:S(2)}, u32[]{:S(2)}) collective-permute-start(f32[4,64,1280]{2,1,0:T(8,128)S(1)} %get-tuple-element.331), channel_id=1, source_target_pairs={{0,4},{1,5},{2,6},{3,7},{4,0},{5,1},{6,2},{7,3},{8,12},{9,13},{10,... | collective-permute-start | bytes 3932168 | tf_op jit(solution)/shard_map/ppermute | solution.py:51
  714.8 70.4 %collective-permute-start.79 = (f32[64,1280]{1,0:T(8,128)S(1)}, f32[64,1280]{1,0:T(8,128)}, u32[]{:S(2)}, u32[]{:S(2)}) collective-permute-start(f32[64,1280]{1,0:T(8,128)S(1)} %get-tuple-element.392), channel_id=1, source_target_pairs={{0,16},{1,17},{2,18},{3,19},{4,20},{5,21},{6,22},{7,23},{8,24},{9,... | collective-permute-start | bytes 983048 | tf_op jit(solution)/shard_map/ppermute | solution.py:51
  716.1 69.2 %collective-permute-start.78 = (f32[64,1280]{1,0:T(8,128)S(1)}, f32[64,1280]{1,0:T(8,128)}, u32[]{:S(2)}, u32[]{:S(2)}) collective-permute-start(f32[64,1280]{1,0:T(8,128)S(1)} %get-tuple-element.393), channel_id=1, source_target_pairs={{0,8},{1,9},{2,10},{3,11},{4,12},{5,13},{6,14},{7,15},{8,0},{9,1},... | collective-permute-start | bytes 983048 | tf_op jit(solution)/shard_map/ppermute | solution.py:51
  718.3 67.0 %collective-permute-start.77 = (f32[64,1280]{1,0:T(8,128)S(1)}, f32[64,1280]{1,0:T(8,128)}, u32[]{:S(2)}, u32[]{:S(2)}) collective-permute-start(f32[64,1280]{1,0:T(8,128)S(1)} %copy-done.41), channel_id=1, source_target_pairs={{0,24},{1,25},{2,26},{3,27},{4,28},{5,29},{6,30},{7,31},{8,16},{9,... | collective-permute-start | bytes 983048 | tf_op jit(solution)/shard_map/ppermute | solution.py:51
  720.2 65.1 %collective-permute-start.76 = (f32[64,1280]{1,0:T(8,128)S(1)}, f32[64,1280]{1,0:T(8,128)}, u32[]{:S(2)}, u32[]{:S(2)}) collective-permute-start(f32[64,1280]{1,0:T(8,128)S(1)} %get-tuple-element.388), channel_id=1, source_target_pairs={{0,16},{1,17},{2,18},{3,19},{4,20},{5,21},{6,22},{7,23},{8,24},{9,... | collective-permute-start | bytes 983048 | tf_op jit(solution)/shard_map/ppermute | solution.py:51
  723.2 62.1 %collective-permute-start.75 = (f32[64,1280]{1,0:T(8,128)S(1)}, f32[64,1280]{1,0:T(8,128)}, u32[]{:S(2)}, u32[]{:S(2)}) collective-permute-start(f32[64,1280]{1,0:T(8,128)S(1)} %get-tuple-element.389), channel_id=1, source_target_pairs={{0,8},{1,9},{2,10},{3,11},{4,12},{5,13},{6,14},{7,15},{8,0},{9,1},... | collective-permute-start | bytes 983048 | tf_op jit(solution)/shard_map/ppermute | solution.py:51
  (158 other events, 3675.6 us)
Sparse Core Ops, SparseCore 0:
  15.7 119.3 all-gather.7
  138.0 115.2 all-gather.9
